TPU v7x, 32 devices: a whole 2x2x4 slice. The times are simulated.
32 devices in a mesh: pipe: 4 (over x, core), mp: 8 (over z, y).
Axes of the slice: x: 2, y: 2, z: 4, core: 2. Of those that a mesh axis runs over, the one named last changes fastest.
Arguments:
- hidden_in: bfloat16 [32, 8192], P(None, 'mp'), may hold values from -24000 to 24000
- lengths: int32 [32], replicated, may hold values from 1 to 256
- assign: int32 [32], replicated, may hold values from 0 to 31, each once
- token_ids: int32 [32], replicated, may hold values from 0 to 12287
- attn_gain: bfloat16 [4, 8192], P('pipe', 'mp'), may hold values from 0.099609375 to 1.8984375
- qkv_weight: bfloat16 [4, 8192, 5120], P('pipe', 'mp'), may hold values from -0.0625 to 0.0625
- qkv_bias: bfloat16 [4, 5120], P('pipe'), may hold values from -3 to 3
- out_weight: bfloat16 [4, 4096, 8192], P('pipe', None, 'mp'), may hold values from -0.375 to 0.375
- kv_cache: bfloat16 [4, 32, 2, 4, 256, 128], P('pipe', 'mp'), may hold values from -120 to 120
- final_gain: bfloat16 [8192], P('mp'), may hold values from 0.099609375 to 1.8984375
- head_weight: bfloat16 [8192, 12288], P(None, ('pipe', 'mp')), may hold values from -0.9923308 to 0.9923308
Outputs:
- logprobs: float32 [32, 12288], P(None, ('pipe', 'mp'))
- chosen: float32 [32], replicated
Inputs may be any that keep to these rules, and one draw needn't show every extreme that they name: `assign`: a permutation of the 32 requests.
All inputs are finite; a program needn't handle non-finite values.
Results may differ from a plain program's by a relative error of at most 0.0017.
Values may be sent and summed in bfloat16 or wider, within the bound.
No kernel may reach another device: no remote copies, remote signals or barrier semaphores. Data moves between devices by JAX's collectives and lax.ppermute only.
A program may use at most 64 MiB of HBM per device.

v0:
```python
import jax
import jax.numpy as jnp
from jax import lax
from jax.sharding import PartitionSpec as P

D = 8192
HEADS = 32
KV_HEADS = 4
HEAD_DIM = 128
MICRO = 4
MB_ROWS = 8
EPS = 1e-06
THETA = 1000000.0


def from_behind(block, axis, distance):
    devices = range(lax.axis_size(axis))
    route = [(i - distance, i) for i in devices if i - distance in devices]
    return lax.ppermute(block, axis, route)


def from_root(value, axis, root):
    mine = lax.axis_index(axis) == root
    return lax.psum(jnp.where(mine, value, jnp.zeros_like(value)), axis)


def rotate(values_in, positions):
    half_dim = values_in.shape[-1] // 2
    frequency = THETA ** (-jnp.arange(half_dim).astype(jnp.float32) * 2.0 / values_in.shape[-1])
    angles = positions.astype(jnp.float32)[:, None, None] * frequency[None, None, :]
    front_half = values_in[..., :half_dim]
    back_half = values_in[..., half_dim:]
    cosine = jnp.cos(angles)
    sine_part = jnp.sin(angles)
    return jnp.concatenate(
        [front_half * cosine - back_half * sine_part, back_half * cosine + front_half * sine_part],
        axis=-1,
    )


def local(
    hidden_in,
    lengths,
    assign,
    token_ids,
    attn_gain,
    qkv_weight,
    qkv_bias,
    out_weight,
    kv_cache,
    final_gain,
    head_weight,
):
    sections = lax.axis_size("pipe")
    section_index = lax.axis_index("pipe")
    local_count = kv_cache.shape[1]
    query_cols = HEADS * HEAD_DIM
    key_cols = KV_HEADS * HEAD_DIM
    group_size = HEADS // KV_HEADS
    scale_factor = HEAD_DIM ** (-0.5)
    own_ids = lax.axis_index("mp") * local_count + jnp.arange(local_count, dtype=jnp.int32)
    slot_ids = jnp.arange(assign.shape[0], dtype=jnp.int32)
    slot_of = jnp.zeros_like(assign).at[assign].set(slot_ids)
    every_row = slot_of % MB_ROWS
    every_batch = slot_of // MB_ROWS
    own_slots = slot_of[own_ids]
    own_lengths = lengths[own_ids]
    own_rows = own_slots % MB_ROWS
    own_batch = own_slots // MB_ROWS
    visible = jnp.arange(kv_cache.shape[4], dtype=jnp.int32)[None, :] < own_lengths[:, None]
    gain_row = attn_gain[0].astype(jnp.float32)
    weight_in = qkv_weight[0]
    bias_row = qkv_bias[0].astype(jnp.float32)
    weight_out = out_weight[0]
    cache_rows = kv_cache[0]
    slot_table = assign.reshape(MICRO, MB_ROWS)
    row_slots = jnp.arange(MB_ROWS, dtype=jnp.int32)

    def attend_one(request_item):
        queries_one, key_one, value_one, cache_one, visible_one, present_one = request_item

        def compute(unused):
            scores = (
                jnp.einsum(
                    "kgd,kjd->kgj", queries_one, cache_one[0], preferred_element_type=jnp.float32
                )
                * scale_factor
            )
            self_score = (
                jnp.einsum("kgd,kd->kg", queries_one, key_one, preferred_element_type=jnp.float32)
                * scale_factor
            )
            key_mask = visible_one[None, None, :]
            row_top = jnp.maximum(jnp.max(jnp.where(key_mask, scores, -1e30), axis=-1), self_score)
            weights = jnp.where(key_mask, jnp.exp(scores - row_top[..., None]), 0.0)
            self_weight = jnp.exp(self_score - row_top)
            row_total = jnp.sum(weights, axis=-1) + self_weight
            summed = jnp.einsum(
                "kgj,kjd->kgd",
                weights.astype(jnp.bfloat16),
                cache_one[1],
                preferred_element_type=jnp.float32,
            )
            summed = summed + jnp.einsum(
                "kg,kd->kgd",
                self_weight.astype(jnp.bfloat16),
                value_one,
                preferred_element_type=jnp.float32,
            )
            return (summed / row_total[..., None]).astype(jnp.bfloat16).reshape(query_cols)

        def nothing(unused):
            return jnp.zeros((query_cols,), jnp.bfloat16)

        return lax.cond(present_one, compute, nothing, 0)

    def apply_layer(rows_in, batch_index):
        current = rows_in.astype(jnp.float32)
        squares = jnp.sum(current * current, axis=1)
        scaled = (current * gain_row).astype(jnp.bfloat16)
        partial_cols = jnp.dot(scaled, weight_in, preferred_element_type=jnp.float32)
        squares_all = lax.psum(squares, "mp")
        share_cols = lax.psum_scatter(partial_cols, "mp", scatter_dimension=1, tiled=True)
        share_width = share_cols.shape[1]
        share_bias = lax.dynamic_slice_in_dim(
            bias_row, lax.axis_index("mp") * share_width, share_width, 0
        )
        share_cols = share_cols * lax.rsqrt(squares_all / D + EPS)[:, None] + share_bias
        wanted = (
            (every_row[:, None] == row_slots[None, :]) & (every_batch[:, None] == batch_index)
        ).astype(jnp.float32)
        routed_rows = jnp.dot(wanted, share_cols, precision=lax.Precision.HIGHEST)
        picked = lax.all_to_all(routed_rows, "mp", split_axis=0, concat_axis=1, tiled=True)
        queries = rotate(
            picked[:, :query_cols].reshape(local_count, HEADS, HEAD_DIM), own_lengths
        ).astype(jnp.bfloat16)
        queries = queries.reshape(local_count, KV_HEADS, group_size, HEAD_DIM)
        key_new = rotate(
            picked[:, query_cols : query_cols + key_cols].reshape(local_count, KV_HEADS, HEAD_DIM),
            own_lengths,
        ).astype(jnp.bfloat16)
        value_new = (
            picked[:, query_cols + key_cols :]
            .reshape(local_count, KV_HEADS, HEAD_DIM)
            .astype(jnp.bfloat16)
        )
        present = own_batch == batch_index
        attended = lax.map(attend_one, (queries, key_new, value_new, cache_rows, visible, present))
        placing = ((own_rows[:, None] == row_slots[None, :]) & present[:, None]).astype(
            jnp.bfloat16
        )
        spread = jnp.dot(placing.T, attended, preferred_element_type=jnp.float32)
        gathered = lax.psum(spread.astype(jnp.bfloat16), "mp")
        update = jnp.dot(gathered, weight_out, preferred_element_type=jnp.float32)
        return (current + update).astype(jnp.bfloat16)

    def advance(turn_index, state_pair):
        outgoing, finished = state_pair
        incoming = from_behind(outgoing, "pipe", 1)
        offset = turn_index - section_index
        batch_index = jnp.clip(offset, 0, MICRO - 1)
        members = lax.dynamic_index_in_dim(slot_table, batch_index, 0, keepdims=False)
        entering = jnp.take(hidden_in, members, axis=0)
        rows_in = jnp.where(section_index == 0, entering, incoming)
        inside = (offset >= 0) & (offset < MICRO)
        rows_out = apply_layer(rows_in, jnp.where(inside, batch_index, -1))
        storing = inside & (section_index == sections - 1)
        placed = lax.dynamic_update_slice_in_dim(finished, rows_out, batch_index * MB_ROWS, 0)
        return (rows_out, jnp.where(storing, placed, finished))

    outgoing = jnp.zeros((MB_ROWS, hidden_in.shape[1]), jnp.bfloat16)
    finished = jnp.zeros(hidden_in.shape, jnp.bfloat16)
    outgoing, finished = lax.fori_loop(0, MICRO + sections - 1, advance, (outgoing, finished))
    final_rows = from_root(finished, "pipe", sections - 1)
    current = final_rows.astype(jnp.float32)
    squares = lax.psum(jnp.sum(current * current, axis=1), "mp")
    normed = (
        current * final_gain.astype(jnp.float32) * lax.rsqrt(squares / D + EPS)[:, None]
    ).astype(jnp.bfloat16)
    logits = jnp.dot(
        lax.all_gather(normed, "mp", axis=1, tiled=True),
        head_weight,
        preferred_element_type=jnp.float32,
    )
    vocab_width = head_weight.shape[1]
    vocab_ids = lax.axis_index(("pipe", "mp")) * vocab_width + jnp.arange(
        vocab_width, dtype=jnp.int32
    )
    targets = token_ids[assign]
    matches = vocab_ids[None, :] == targets[:, None]
    picked_local = jnp.sum(jnp.where(matches, logits, 0.0), axis=1)
    local_top = jnp.max(logits, axis=1)
    row_top = lax.pmax(local_top, ("pipe", "mp"))
    local_total = jnp.sum(jnp.exp(logits - row_top[:, None]), axis=1)
    row_total, picked = lax.psum((local_total, picked_local), ("pipe", "mp"))
    log_total = row_top + jnp.log(row_total)
    return (logits - log_total[:, None], picked - log_total)


def solution(mesh):
    return jax.shard_map(
        local,
        mesh=mesh,
        in_specs=(
            P(None, "mp"),
            P(),
            P(),
            P(),
            P("pipe", "mp"),
            P("pipe", "mp", None),
            P("pipe", None),
            P("pipe", None, "mp"),
            P("pipe", "mp", None, None, None, None),
            P("mp"),
            P(None, ("pipe", "mp")),
        ),
        out_specs=(P(None, ("pipe", "mp")), P()),
        check_vma=False,
    )
```

profile of v0, /device:TPU:0, one launch (start us, length us, event | category | flops | bytes accessed | tf_op | source)
XLA Modules:
  0.0 1336.8 jit_solution(10831050884700243807)
XLA Ops:
  13.6 1144.0 %while.53 = (s32[]{:T(128)}, bf16[8,1024]{1,0:T(8,128)(2,1)S(1)}, bf16[32,1024]{1,0:T(8,128)(2,1)S(1)}, pred[]{:T(512)}, s32[]{:T(128)}, /*index=5*/s32[4,8]{1,0...) while((s32[]{:T(128)}, bf16[8,1024]{1,0:T(8,128)(2,1)S(1)}, ...), condition=%wide.region_12.13_spmd.clone.clone, body=%wide.region_1.12_spmd.clone.clone.sunk | while | flops 157849424 | bytes 22136348 | solution.py:173
  24.2 22.5 %psum.66 = f32[8]{0:T(128)S(1)} all-reduce(f32[8]{0:T(128)S(1)} %get-tuple-element.929), channel_id=1, replica_groups=mesh['pipe'=4,'mp'=8] {'mp'}, use_global_device_ids=true, to_apply=%region_4.4 | all-reduce | flops 8 | bytes 64 | tf_op jit(solution)/shard_map/while/body/eval_jaxpr/psum | solution.py:122
  46.7 36.4 %reduce-scatter.2.cloned.1.call-done = f32[8,640]{1,0:T(8,128)} async-done(((f32[8,5120]{1,0:T(8,128)}), f32[8,640]{1,0:T(8,128)}) %reduce-scatter.2.cloned.1.call-update) | async-done | bytes 20496 | tf_op jit(solution)/shard_map/while/body/eval_jaxpr/reduce_scatter | solution.py:123
  108.5 65.4 %all-reduce.6.cloned.1.call-done = bf16[8,4096]{1,0:T(8,128)(2,1)} async-done(((bf16[8,4096]{1,0:T(8,128)(2,1)}), bf16[8,4096]{1,0:T(8,128)(2,1)}) %all-reduce.6.cloned.1.call-update) | async-done | bytes 65552 | tf_op jit(solution)/shard_map/while/body/eval_jaxpr/psum | solution.py:153
  188.0 20.4 %psum.66 = f32[8]{0:T(128)S(1)} all-reduce(f32[8]{0:T(128)S(1)} %get-tuple-element.929), channel_id=1, replica_groups=mesh['pipe'=4,'mp'=8] {'mp'}, use_global_device_ids=true, to_apply=%region_4.4 | all-reduce | flops 8 | bytes 64 | tf_op jit(solution)/shard_map/while/body/eval_jaxpr/psum | solution.py:122
  208.4 36.8 %reduce-scatter.2.cloned.1.call-done = f32[8,640]{1,0:T(8,128)} async-done(((f32[8,5120]{1,0:T(8,128)}), f32[8,640]{1,0:T(8,128)}) %reduce-scatter.2.cloned.1.call-update) | async-done | bytes 20496 | tf_op jit(solution)/shard_map/while/body/eval_jaxpr/reduce_scatter | solution.py:123
  270.7 65.3 %all-reduce.6.cloned.1.call-done = bf16[8,4096]{1,0:T(8,128)(2,1)} async-done(((bf16[8,4096]{1,0:T(8,128)(2,1)}), bf16[8,4096]{1,0:T(8,128)(2,1)}) %all-reduce.6.cloned.1.call-update) | async-done | bytes 65552 | tf_op jit(solution)/shard_map/while/body/eval_jaxpr/psum | solution.py:153
  350.0 20.4 %psum.66 = f32[8]{0:T(128)S(1)} all-reduce(f32[8]{0:T(128)S(1)} %get-tuple-element.929), channel_id=1, replica_groups=mesh['pipe'=4,'mp'=8] {'mp'}, use_global_device_ids=true, to_apply=%region_4.4 | all-reduce | flops 8 | bytes 64 | tf_op jit(solution)/shard_map/while/body/eval_jaxpr/psum | solution.py:122
  370.4 36.8 %reduce-scatter.2.cloned.1.call-done = f32[8,640]{1,0:T(8,128)} async-done(((f32[8,5120]{1,0:T(8,128)}), f32[8,640]{1,0:T(8,128)}) %reduce-scatter.2.cloned.1.call-update) | async-done | bytes 20496 | tf_op jit(solution)/shard_map/while/body/eval_jaxpr/reduce_scatter | solution.py:123
  427.2 73.7 %all-reduce.6.cloned.1.call-done = bf16[8,4096]{1,0:T(8,128)(2,1)} async-done(((bf16[8,4096]{1,0:T(8,128)(2,1)}), bf16[8,4096]{1,0:T(8,128)(2,1)}) %all-reduce.6.cloned.1.call-update) | async-done | bytes 65552 | tf_op jit(solution)/shard_map/while/body/eval_jaxpr/psum | solution.py:153
  515.0 20.4 %psum.66 = f32[8]{0:T(128)S(1)} all-reduce(f32[8]{0:T(128)S(1)} %get-tuple-element.929), channel_id=1, replica_groups=mesh['pipe'=4,'mp'=8] {'mp'}, use_global_device_ids=true, to_apply=%region_4.4 | all-reduce | flops 8 | bytes 64 | tf_op jit(solution)/shard_map/while/body/eval_jaxpr/psum | solution.py:122
  535.3 36.8 %reduce-scatter.2.cloned.1.call-done = f32[8,640]{1,0:T(8,128)} async-done(((f32[8,5120]{1,0:T(8,128)}), f32[8,640]{1,0:T(8,128)}) %reduce-scatter.2.cloned.1.call-update) | async-done | bytes 20496 | tf_op jit(solution)/shard_map/while/body/eval_jaxpr/reduce_scatter | solution.py:123
  592.1 72.1 %all-reduce.6.cloned.1.call-done = bf16[8,4096]{1,0:T(8,128)(2,1)} async-done(((bf16[8,4096]{1,0:T(8,128)(2,1)}), bf16[8,4096]{1,0:T(8,128)(2,1)}) %all-reduce.6.cloned.1.call-update) | async-done | bytes 65552 | tf_op jit(solution)/shard_map/while/body/eval_jaxpr/psum | solution.py:153
  698.7 36.8 %reduce-scatter.2.cloned.1.call-done = f32[8,640]{1,0:T(8,128)} async-done(((f32[8,5120]{1,0:T(8,128)}), f32[8,640]{1,0:T(8,128)}) %reduce-scatter.2.cloned.1.call-update) | async-done | bytes 20496 | tf_op jit(solution)/shard_map/while/body/eval_jaxpr/reduce_scatter | solution.py:123
  755.5 74.6 %all-reduce.6.cloned.1.call-done = bf16[8,4096]{1,0:T(8,128)(2,1)} async-done(((bf16[8,4096]{1,0:T(8,128)(2,1)}), bf16[8,4096]{1,0:T(8,128)(2,1)}) %all-reduce.6.cloned.1.call-update) | async-done | bytes 65552 | tf_op jit(solution)/shard_map/while/body/eval_jaxpr/psum | solution.py:153
  864.5 36.8 %reduce-scatter.2.cloned.1.call-done = f32[8,640]{1,0:T(8,128)} async-done(((f32[8,5120]{1,0:T(8,128)}), f32[8,640]{1,0:T(8,128)}) %reduce-scatter.2.cloned.1.call-update) | async-done | bytes 20496 | tf_op jit(solution)/shard_map/while/body/eval_jaxpr/reduce_scatter | solution.py:123
  921.3 72.2 %all-reduce.6.cloned.1.call-done = bf16[8,4096]{1,0:T(8,128)(2,1)} async-done(((bf16[8,4096]{1,0:T(8,128)(2,1)}), bf16[8,4096]{1,0:T(8,128)(2,1)}) %all-reduce.6.cloned.1.call-update) | async-done | bytes 65552 | tf_op jit(solution)/shard_map/while/body/eval_jaxpr/psum | solution.py:153
  1028.0 36.8 %reduce-scatter.2.cloned.1.call-done = f32[8,640]{1,0:T(8,128)} async-done(((f32[8,5120]{1,0:T(8,128)}), f32[8,640]{1,0:T(8,128)}) %reduce-scatter.2.cloned.1.call-update) | async-done | bytes 20496 | tf_op jit(solution)/shard_map/while/body/eval_jaxpr/reduce_scatter | solution.py:123
  1084.8 68.2 %all-reduce.6.cloned.1.call-done = bf16[8,4096]{1,0:T(8,128)(2,1)} async-done(((bf16[8,4096]{1,0:T(8,128)(2,1)}), bf16[8,4096]{1,0:T(8,128)(2,1)}) %all-reduce.6.cloned.1.call-update) | async-done | bytes 65552 | tf_op jit(solution)/shard_map/while/body/eval_jaxpr/psum | solution.py:153
  1159.0 32.6 %all-reduce.4.cloned.1.call-done = bf16[32,1024]{1,0:T(8,128)(2,1)} async-done(((bf16[32,1024]{1,0:T(8,128)(2,1)}), bf16[32,1024]{1,0:T(8,128)(2,1)}) %all-reduce.4.cloned.1.call-update) | async-done | bytes 65552 | tf_op jit(solution)/shard_map/psum | solution.py:24
  1192.6 21.4 %psum.57 = f32[32]{0:T(128)S(1)} all-reduce(f32[32]{0:T(128)S(1)} %fusion.50), channel_id=1, replica_groups=mesh['pipe'=4,'mp'=8] {'mp'}, use_global_device_ids=true, to_apply=%region_15.16 | all-reduce | flops 32 | bytes 256 | tf_op jit(solution)/shard_map/psum | solution.py:176
  1214.9 31.4 %all_gather.3 = bf16[32,8192]{1,0:T(8,128)(2,1)S(1)} all-gather(bf16[32,1024]{1,0:T(8,128)(2,1)S(1)} %fusion.49), channel_id=1, replica_groups=mesh['pipe'=4,'mp'=8] {'mp'}, dimensions={1}, use_global_device_ids=true | all-gather | bytes 589824 | tf_op jit(solution)/shard_map/all_gather | solution.py:181
  1250.2 36.8 %pmax.7 = f32[32]{0:T(128)S(1)} all-reduce(f32[32]{0:T(128)S(1)} %get-tuple-element.743), channel_id=1, replica_groups=mesh['pipe'=4,'mp'=8] {'pipe','mp'}, use_global_device_ids=true, to_apply=%region_17.18 | all-reduce | flops 32 | bytes 256 | tf_op jit(solution)/shard_map/pmax | solution.py:193
  1287.3 41.2 %all-reduce = (f32[32]{0:T(128)S(1)}, f32[32]{0:T(128)S(1)}) all-reduce(f32[32]{0:T(128)S(1)} %get-tuple-element.666, f32[32]{0:T(128)S(1)} %get-tuple-element.665), channel_id=1, replica_groups=mesh['pipe'=4,'mp'=8] {'pipe','mp'}, use_global_device_ids=true, to_apply=%region_19.20 | all-reduce | flops 64 | bytes 512 | tf_op jit(solution)/shard_map/psum | solution.py:195
  (450 shorter events, 370.7 us)
Async XLA Ops:
  13.6 69.5 %reduce-scatter.2.cloned.1.call-start = ((), (), s32[]{:S(2)}) async-start(), calls=%async_computation.3 | async-start | bytes 184320 | tf_op jit(solution)/shard_map/while/body/eval_jaxpr/reduce_scatter | solution.py:123
  13.7 4.1 collective-permute-start
  84.7 10.6 all-to-all-start
  88.3 85.6 %all-reduce.6.cloned.1.call-start = ((), (), s32[]{:S(2)}) async-start(), calls=%async_computation.4 | async-start | bytes 131072 | tf_op jit(solution)/shard_map/while/body/eval_jaxpr/psum | solution.py:153
  178.5 66.7 %reduce-scatter.2.cloned.1.call-start = ((), (), s32[]{:S(2)}) async-start(), calls=%async_computation.3 | async-start | bytes 184320 | tf_op jit(solution)/shard_map/while/body/eval_jaxpr/reduce_scatter | solution.py:123
  246.8 10.6 all-to-all-start
  250.4 85.5 %all-reduce.6.cloned.1.call-start = ((), (), s32[]{:S(2)}) async-start(), calls=%async_computation.4 | async-start | bytes 131072 | tf_op jit(solution)/shard_map/while/body/eval_jaxpr/psum | solution.py:153
  340.5 66.7 %reduce-scatter.2.cloned.1.call-start = ((), (), s32[]{:S(2)}) async-start(), calls=%async_computation.3 | async-start | bytes 184320 | tf_op jit(solution)/shard_map/while/body/eval_jaxpr/reduce_scatter | solution.py:123
  408.8 10.6 all-to-all-start
  412.4 88.4 %all-reduce.6.cloned.1.call-start = ((), (), s32[]{:S(2)}) async-start(), calls=%async_computation.4 | async-start | bytes 131072 | tf_op jit(solution)/shard_map/while/body/eval_jaxpr/psum | solution.py:153
  505.5 66.7 %reduce-scatter.2.cloned.1.call-start = ((), (), s32[]{:S(2)}) async-start(), calls=%async_computation.3 | async-start | bytes 184320 | tf_op jit(solution)/shard_map/while/body/eval_jaxpr/reduce_scatter | solution.py:123
  505.5 3.0 collective-permute-start
  573.8 10.6 all-to-all-start
  577.4 86.8 %all-reduce.6.cloned.1.call-start = ((), (), s32[]{:S(2)}) async-start(), calls=%async_computation.4 | async-start | bytes 131072 | tf_op jit(solution)/shard_map/while/body/eval_jaxpr/psum | solution.py:153
  668.8 66.7 %reduce-scatter.2.cloned.1.call-start = ((), (), s32[]{:S(2)}) async-start(), calls=%async_computation.3 | async-start | bytes 184320 | tf_op jit(solution)/shard_map/while/body/eval_jaxpr/reduce_scatter | solution.py:123
  737.1 10.6 all-to-all-start
  740.7 89.3 %all-reduce.6.cloned.1.call-start = ((), (), s32[]{:S(2)}) async-start(), calls=%async_computation.4 | async-start | bytes 131072 | tf_op jit(solution)/shard_map/while/body/eval_jaxpr/psum | solution.py:153
  834.7 66.7 %reduce-scatter.2.cloned.1.call-start = ((), (), s32[]{:S(2)}) async-start(), calls=%async_computation.3 | async-start | bytes 184320 | tf_op jit(solution)/shard_map/while/body/eval_jaxpr/reduce_scatter | solution.py:123
  902.9 10.6 all-to-all-start
  906.6 86.9 %all-reduce.6.cloned.1.call-start = ((), (), s32[]{:S(2)}) async-start(), calls=%async_computation.4 | async-start | bytes 131072 | tf_op jit(solution)/shard_map/while/body/eval_jaxpr/psum | solution.py:153
  998.1 66.7 %reduce-scatter.2.cloned.1.call-start = ((), (), s32[]{:S(2)}) async-start(), calls=%async_computation.3 | async-start | bytes 184320 | tf_op jit(solution)/shard_map/while/body/eval_jaxpr/reduce_scatter | solution.py:123
  1066.4 10.6 all-to-all-start
  1070.0 83.0 %all-reduce.6.cloned.1.call-start = ((), (), s32[]{:S(2)}) async-start(), calls=%async_computation.4 | async-start | bytes 131072 | tf_op jit(solution)/shard_map/while/body/eval_jaxpr/psum | solution.py:153
  1157.6 34.1 %all-reduce.4.cloned.1.call-start = ((), (), s32[]{:S(2)}) async-start(), calls=%async_computation.2 | async-start | bytes 131072 | tf_op jit(solution)/shard_map/psum | solution.py:24
  (7 other events, 2310.1 us)
Sparse Core Ops, SparseCore 0:
  24.2 58.8 reduce-scatter.1
  108.6 65.2 all-reduce.5
  188.0 57.1 reduce-scatter.1
  270.8 65.1 all-reduce.5
  350.0 57.1 reduce-scatter.1
  427.3 73.5 all-reduce.5
  515.0 57.1 reduce-scatter.1
  592.2 71.9 all-reduce.5
  678.3 57.1 reduce-scatter.1
  755.6 74.4 all-reduce.5
  844.1 57.1 reduce-scatter.1
  921.4 72.0 all-reduce.5
  1007.6 57.1 reduce-scatter.1
  1084.9 68.0 all-reduce.5
Sparse Core Ops, SparseCore 1:
  1160.4 31.2 all-reduce.3
where the time goes:
time: 1340 us
  waiting for transfers between devices  830 us (62%)
  blocking collectives  276 us (21%)
  matrix products  102 us (8%)
  local copies, waits for them, and re-layouts  43.2 us (3%)
  starting transfers between devices  35.9 us (3%)
  loops' own time  22.4 us (2%)
  between operations  15.3 us (1%)
    psum x7, waiting for transfers between devices, apply_layer(): gathered = lax.psum(spread.astype(jnp.bfloat16), 'mp')  491 us
    reduce_scatter x7, waiting for transfers between devices, apply_layer(): lax.psum_scatter(partial_cols, 'mp', scatter_dimension=1, tiled=True)  257 us
    psum x7, blocking collectives, apply_layer(): squares_all = lax.psum(squares, 'mp')  145 us
    all_to_all x7, waiting for transfers between devices, apply_layer(): lax.all_to_all(routed_rows, 'mp', split_axis=0, concat_axis=1, tiled=True)  48.7 us
    dot_general x7, matrix products, apply_layer(): jnp.dot(scaled, weight_in, preferred_element_type=jnp.float32)  42.7 us
    psum x1, blocking collectives, local(): row_total, picked = lax.psum((local_total, picked_local), ('pipe', 'mp'))  41.2 us
    pmax x1, blocking collectives, local(): row_top = lax.pmax(local_top, ('pipe', 'mp'))  36.8 us
    psum x1, waiting for transfers between devices, from_root(): return lax.psum(jnp.where(mine, value, jnp.zeros_like(value)), axis)  32.6 us
  transfers between devices with their start and end apart: 29, of which 22 were waited for; matrix products, arithmetic and copies ran while one was open for 1% of the time, Pallas kernels for 0%

commit v1 on v0

--- a/solution.py
+++ b/solution.py
@@ -150,7 +150,7 @@
             jnp.bfloat16
         )
         spread = jnp.dot(placing.T, attended, preferred_element_type=jnp.float32)
-        gathered = lax.psum(spread.astype(jnp.bfloat16), "mp")
+        gathered = jnp.sum(lax.all_gather(spread.astype(jnp.bfloat16), "mp"), axis=0)
         update = jnp.dot(gathered, weight_out, preferred_element_type=jnp.float32)
         return (current + update).astype(jnp.bfloat16)
 

time: 1340 us -> 1060 us (0.79)
  waiting for transfers between devices: 830 us -> 341 us
  blocking collectives: 276 us -> 491 us
    psum x7 -> x0, waiting for transfers between devices: 491 us -> none  [apply_layer(): gathered = lax.psum(spread.astype(jnp.bfloat16), 'mp')]
    all_gather x0 -> x7, blocking collectives: none -> 225 us  [apply_layer(): lax.all_gather(spread.astype(jnp.bfloat16), 'mp')]
  transfers between devices with their start and end apart: 29 -> 22, of which waited for: 22 -> 15; matrix products, arithmetic and copies ran while one was open for 1% -> 1% of each run, Pallas kernels for 0% -> 0%
where the time goes in v1:
time: 1060 us
  blocking collectives  491 us (46%)
  waiting for transfers between devices  341 us (32%)
  matrix products  97.3 us (9%)
  local copies, waits for them, and re-layouts  43.2 us (4%)
  starting transfers between devices  35.7 us (3%)
  loops' own time  22.3 us (2%)
  between operations  15.6 us (1%)
  other arithmetic  12.8 us (1%)
    reduce_scatter x7, waiting for transfers between devices, apply_layer(): lax.psum_scatter(partial_cols, 'mp', scatter_dimension=1, tiled=True)  262 us
    all_gather x7, blocking collectives, apply_layer(): lax.all_gather(spread.astype(jnp.bfloat16), 'mp')  225 us
    psum x7, blocking collectives, apply_layer(): squares_all = lax.psum(squares, 'mp')  135 us
    all_to_all x7, waiting for transfers between devices, apply_layer(): lax.all_to_all(routed_rows, 'mp', split_axis=0, concat_axis=1, tiled=True)  49.1 us
    dot_general x7, matrix products, apply_layer(): jnp.dot(scaled, weight_in, preferred_element_type=jnp.float32)  42.7 us
    psum x1, blocking collectives, local(): row_total, picked = lax.psum((local_total, picked_local), ('pipe', 'mp'))  41.2 us
    pmax x1, blocking collectives, local(): row_top = lax.pmax(local_top, ('pipe', 'mp'))  36.9 us
    dot_general x7, matrix products, apply_layer(): update = jnp.dot(gathered, weight_out, preferred_element_type=jnp.float32)  32.1 us
  transfers between devices with their start and end apart: 22, of which 15 were waited for; matrix products, arithmetic and copies ran while one was open for 1% of the time, Pallas kernels for 0%

profile of v1, /device:TPU:0, one launch (start us, length us, event | category | flops | bytes accessed | tf_op | source)
XLA Modules:
  0.0 1059.0 jit_solution(7733927840864328642)
XLA Ops:
  13.6 868.2 %while.53 = (s32[]{:T(128)}, bf16[8,1024]{1,0:T(8,128)(2,1)S(1)}, bf16[32,1024]{1,0:T(8,128)(2,1)S(1)}, pred[]{:T(512)}, s32[]{:T(128)}, /*index=5*/s32[4,8]{1,0...) while((s32[]{:T(128)}, bf16[8,1024]{1,0:T(8,128)(2,1)S(1)}, ...), condition=%wide.region_12.13_spmd.clone.clone, body=%wide.region_1.12_spmd.clone.clone.sunk | while | flops 158046032 | bytes 22922740 | solution.py:173
  24.2 22.5 %psum.49 = f32[8]{0:T(128)S(1)} all-reduce(f32[8]{0:T(128)S(1)} %get-tuple-element.930), channel_id=1, replica_groups=mesh['pipe'=4,'mp'=8] {'mp'}, use_global_device_ids=true, to_apply=%region_4.4 | all-reduce | flops 8 | bytes 64 | tf_op jit(solution)/shard_map/while/body/eval_jaxpr/psum | solution.py:122
  46.7 36.4 %reduce-scatter.2.cloned.1.call-done = f32[8,640]{1,0:T(8,128)} async-done(((f32[8,5120]{1,0:T(8,128)}), f32[8,640]{1,0:T(8,128)}) %reduce-scatter.2.cloned.1.call-update) | async-done | bytes 20496 | tf_op jit(solution)/shard_map/while/body/eval_jaxpr/reduce_scatter | solution.py:123
  107.9 31.3 %all-gather.3 = bf16[64,4096]{1,0:T(8,128)(2,1)S(1)} all-gather(bf16[8,4096]{1,0:T(8,128)(2,1)S(1)} %convolution_convert_fusion.2), channel_id=2, replica_groups=mesh['pipe'=4,'mp'=8] {'mp'}, dimensions={0}, use_global_device_ids=true | all-gather | bytes 589824 | tf_op jit(solution)/shard_map/while/body/eval_jaxpr/all_gather | solution.py:153
  170.6 34.2 %reduce-scatter.2.cloned.1.call-done = f32[8,640]{1,0:T(8,128)} async-done(((f32[8,5120]{1,0:T(8,128)}), f32[8,640]{1,0:T(8,128)}) %reduce-scatter.2.cloned.1.call-update) | async-done | bytes 20496 | tf_op jit(solution)/shard_map/while/body/eval_jaxpr/reduce_scatter | solution.py:123
  229.6 31.3 %all-gather.3 = bf16[64,4096]{1,0:T(8,128)(2,1)S(1)} all-gather(bf16[8,4096]{1,0:T(8,128)(2,1)S(1)} %convolution_convert_fusion.2), channel_id=2, replica_groups=mesh['pipe'=4,'mp'=8] {'mp'}, dimensions={0}, use_global_device_ids=true | all-gather | bytes 589824 | tf_op jit(solution)/shard_map/while/body/eval_jaxpr/all_gather | solution.py:153
  292.5 34.1 %reduce-scatter.2.cloned.1.call-done = f32[8,640]{1,0:T(8,128)} async-done(((f32[8,5120]{1,0:T(8,128)}), f32[8,640]{1,0:T(8,128)}) %reduce-scatter.2.cloned.1.call-update) | async-done | bytes 20496 | tf_op jit(solution)/shard_map/while/body/eval_jaxpr/reduce_scatter | solution.py:123
  345.9 35.2 %all-gather.3 = bf16[64,4096]{1,0:T(8,128)(2,1)S(1)} all-gather(bf16[8,4096]{1,0:T(8,128)(2,1)S(1)} %convolution_convert_fusion.2), channel_id=2, replica_groups=mesh['pipe'=4,'mp'=8] {'mp'}, dimensions={0}, use_global_device_ids=true | all-gather | bytes 589824 | tf_op jit(solution)/shard_map/while/body/eval_jaxpr/all_gather | solution.py:153
  395.2 21.8 %psum.49 = f32[8]{0:T(128)S(1)} all-reduce(f32[8]{0:T(128)S(1)} %get-tuple-element.930), channel_id=1, replica_groups=mesh['pipe'=4,'mp'=8] {'mp'}, use_global_device_ids=true, to_apply=%region_4.4 | all-reduce | flops 8 | bytes 64 | tf_op jit(solution)/shard_map/while/body/eval_jaxpr/psum | solution.py:122
  417.0 34.2 %reduce-scatter.2.cloned.1.call-done = f32[8,640]{1,0:T(8,128)} async-done(((f32[8,5120]{1,0:T(8,128)}), f32[8,640]{1,0:T(8,128)}) %reduce-scatter.2.cloned.1.call-update) | async-done | bytes 20496 | tf_op jit(solution)/shard_map/while/body/eval_jaxpr/reduce_scatter | solution.py:123
  470.5 32.3 %all-gather.3 = bf16[64,4096]{1,0:T(8,128)(2,1)S(1)} all-gather(bf16[8,4096]{1,0:T(8,128)(2,1)S(1)} %convolution_convert_fusion.2), channel_id=2, replica_groups=mesh['pipe'=4,'mp'=8] {'mp'}, dimensions={0}, use_global_device_ids=true | all-gather | bytes 589824 | tf_op jit(solution)/shard_map/while/body/eval_jaxpr/all_gather | solution.py:153
  517.0 20.3 %psum.49 = f32[8]{0:T(128)S(1)} all-reduce(f32[8]{0:T(128)S(1)} %get-tuple-element.930), channel_id=1, replica_groups=mesh['pipe'=4,'mp'=8] {'mp'}, use_global_device_ids=true, to_apply=%region_4.4 | all-reduce | flops 8 | bytes 64 | tf_op jit(solution)/shard_map/while/body/eval_jaxpr/psum | solution.py:122
  537.3 38.9 %reduce-scatter.2.cloned.1.call-done = f32[8,640]{1,0:T(8,128)} async-done(((f32[8,5120]{1,0:T(8,128)}), f32[8,640]{1,0:T(8,128)}) %reduce-scatter.2.cloned.1.call-update) | async-done | bytes 20496 | tf_op jit(solution)/shard_map/while/body/eval_jaxpr/reduce_scatter | solution.py:123
  595.5 31.8 %all-gather.3 = bf16[64,4096]{1,0:T(8,128)(2,1)S(1)} all-gather(bf16[8,4096]{1,0:T(8,128)(2,1)S(1)} %convolution_convert_fusion.2), channel_id=2, replica_groups=mesh['pipe'=4,'mp'=8] {'mp'}, dimensions={0}, use_global_device_ids=true | all-gather | bytes 589824 | tf_op jit(solution)/shard_map/while/body/eval_jaxpr/all_gather | solution.py:153
  659.2 44.1 %reduce-scatter.2.cloned.1.call-done = f32[8,640]{1,0:T(8,128)} async-done(((f32[8,5120]{1,0:T(8,128)}), f32[8,640]{1,0:T(8,128)}) %reduce-scatter.2.cloned.1.call-update) | async-done | bytes 20496 | tf_op jit(solution)/shard_map/while/body/eval_jaxpr/reduce_scatter | solution.py:123
  722.6 31.5 %all-gather.3 = bf16[64,4096]{1,0:T(8,128)(2,1)S(1)} all-gather(bf16[8,4096]{1,0:T(8,128)(2,1)S(1)} %convolution_convert_fusion.2), channel_id=2, replica_groups=mesh['pipe'=4,'mp'=8] {'mp'}, dimensions={0}, use_global_device_ids=true | all-gather | bytes 589824 | tf_op jit(solution)/shard_map/while/body/eval_jaxpr/all_gather | solution.py:153
  768.3 18.0 %psum.49 = f32[8]{0:T(128)S(1)} all-reduce(f32[8]{0:T(128)S(1)} %get-tuple-element.930), channel_id=1, replica_groups=mesh['pipe'=4,'mp'=8] {'mp'}, use_global_device_ids=true, to_apply=%region_4.4 | all-reduce | flops 8 | bytes 64 | tf_op jit(solution)/shard_map/while/body/eval_jaxpr/psum | solution.py:122
  786.3 40.0 %reduce-scatter.2.cloned.1.call-done = f32[8,640]{1,0:T(8,128)} async-done(((f32[8,5120]{1,0:T(8,128)}), f32[8,640]{1,0:T(8,128)}) %reduce-scatter.2.cloned.1.call-update) | async-done | bytes 20496 | tf_op jit(solution)/shard_map/while/body/eval_jaxpr/reduce_scatter | solution.py:123
  845.6 31.5 %all-gather.3 = bf16[64,4096]{1,0:T(8,128)(2,1)S(1)} all-gather(bf16[8,4096]{1,0:T(8,128)(2,1)S(1)} %convolution_convert_fusion.2), channel_id=2, replica_groups=mesh['pipe'=4,'mp'=8] {'mp'}, dimensions={0}, use_global_device_ids=true | all-gather | bytes 589824 | tf_op jit(solution)/shard_map/while/body/eval_jaxpr/all_gather | solution.py:153
  883.2 30.3 %all-reduce.3.cloned.1.call-done = bf16[32,1024]{1,0:T(8,128)(2,1)} async-done(((bf16[32,1024]{1,0:T(8,128)(2,1)}), bf16[32,1024]{1,0:T(8,128)(2,1)}) %all-reduce.3.cloned.1.call-update) | async-done | bytes 65552 | tf_op jit(solution)/shard_map/psum | solution.py:24
  914.5 21.4 %psum.43 = f32[32]{0:T(128)S(1)} all-reduce(f32[32]{0:T(128)S(1)} %fusion.50), channel_id=1, replica_groups=mesh['pipe'=4,'mp'=8] {'mp'}, use_global_device_ids=true, to_apply=%region_15.16 | all-reduce | flops 32 | bytes 256 | tf_op jit(solution)/shard_map/psum | solution.py:176
  936.8 31.4 %all_gather.23 = bf16[32,8192]{1,0:T(8,128)(2,1)S(1)} all-gather(bf16[32,1024]{1,0:T(8,128)(2,1)S(1)} %fusion.49), channel_id=1, replica_groups=mesh['pipe'=4,'mp'=8] {'mp'}, dimensions={1}, use_global_device_ids=true | all-gather | bytes 589824 | tf_op jit(solution)/shard_map/all_gather | solution.py:181
  972.1 36.9 %pmax.7 = f32[32]{0:T(128)S(1)} all-reduce(f32[32]{0:T(128)S(1)} %get-tuple-element.744), channel_id=1, replica_groups=mesh['pipe'=4,'mp'=8] {'pipe','mp'}, use_global_device_ids=true, to_apply=%region_17.18 | all-reduce | flops 32 | bytes 256 | tf_op jit(solution)/shard_map/pmax | solution.py:193
  1009.1 41.2 %all-reduce = (f32[32]{0:T(128)S(1)}, f32[32]{0:T(128)S(1)}) all-reduce(f32[32]{0:T(128)S(1)} %get-tuple-element.667, f32[32]{0:T(128)S(1)} %get-tuple-element.666), channel_id=1, replica_groups=mesh['pipe'=4,'mp'=8] {'pipe','mp'}, use_global_device_ids=true, to_apply=%region_19.20 | all-reduce | flops 64 | bytes 512 | tf_op jit(solution)/shard_map/psum | solution.py:195
  (443 shorter events, 357.9 us)
Async XLA Ops:
  8.0 874.5 %copy-start = (s32[32]{0:T(128)S(1)}, s32[32]{0:T(128)}, u32[]{:S(2)}) copy-start(s32[32]{0:T(128)} %param.20) | copy-start | bytes 388
  13.6 868.9 %copy-start.1 = (bf16[1024]{0:T(1024)(128)(2,1)S(1)}, bf16[1024]{0:T(1024)(128)(2,1)}, u32[]{:S(2)}) copy-start(bf16[1024]{0:T(1024)(128)(2,1)} %param.26) | copy-start | bytes 6148
  13.6 69.5 %reduce-scatter.2.cloned.1.call-start = ((), (), s32[]{:S(2)}) async-start(), calls=%async_computation.3 | async-start | bytes 184320 | tf_op jit(solution)/shard_map/while/body/eval_jaxpr/reduce_scatter | solution.py:123
  13.7 4.1 collective-permute-start
  84.7 10.6 %all-to-all-start = ((f32[8,4,640]{2,1,0:T(4,128)}), f32[8,4,640]{2,1,0:T(4,128)S(1)}, u32[]{:S(2)}, u32[]{:S(2)}) async-start(f32[8,4,640]{2,1,0:T(4,128)} %all_to_all.47), calls=%async_computation.1 | async-start | bytes 163840 | tf_op jit(solution)/shard_map/while/body/eval_jaxpr/all_to_all | solution.py:133
  143.8 61.0 %reduce-scatter.2.cloned.1.call-start = ((), (), s32[]{:S(2)}) async-start(), calls=%async_computation.3 | async-start | bytes 184320 | tf_op jit(solution)/shard_map/while/body/eval_jaxpr/reduce_scatter | solution.py:123
  143.8 3.0 collective-permute-start
  206.4 10.6 %all-to-all-start = ((f32[8,4,640]{2,1,0:T(4,128)}), f32[8,4,640]{2,1,0:T(4,128)S(1)}, u32[]{:S(2)}, u32[]{:S(2)}) async-start(f32[8,4,640]{2,1,0:T(4,128)} %all_to_all.47), calls=%async_computation.1 | async-start | bytes 163840 | tf_op jit(solution)/shard_map/while/body/eval_jaxpr/all_to_all | solution.py:133
  265.6 61.0 %reduce-scatter.2.cloned.1.call-start = ((), (), s32[]{:S(2)}) async-start(), calls=%async_computation.3 | async-start | bytes 184320 | tf_op jit(solution)/shard_map/while/body/eval_jaxpr/reduce_scatter | solution.py:123
  265.6 3.0 collective-permute-start
  328.2 10.6 %all-to-all-start = ((f32[8,4,640]{2,1,0:T(4,128)}), f32[8,4,640]{2,1,0:T(4,128)S(1)}, u32[]{:S(2)}, u32[]{:S(2)}) async-start(f32[8,4,640]{2,1,0:T(4,128)} %all_to_all.47), calls=%async_computation.1 | async-start | bytes 163840 | tf_op jit(solution)/shard_map/while/body/eval_jaxpr/all_to_all | solution.py:133
  385.7 65.5 %reduce-scatter.2.cloned.1.call-start = ((), (), s32[]{:S(2)}) async-start(), calls=%async_computation.3 | async-start | bytes 184320 | tf_op jit(solution)/shard_map/while/body/eval_jaxpr/reduce_scatter | solution.py:123
  385.7 3.0 collective-permute-start
  452.8 10.7 %all-to-all-start = ((f32[8,4,640]{2,1,0:T(4,128)}), f32[8,4,640]{2,1,0:T(4,128)S(1)}, u32[]{:S(2)}, u32[]{:S(2)}) async-start(f32[8,4,640]{2,1,0:T(4,128)} %all_to_all.47), calls=%async_computation.1 | async-start | bytes 163840 | tf_op jit(solution)/shard_map/while/body/eval_jaxpr/all_to_all | solution.py:133
  507.5 68.7 %reduce-scatter.2.cloned.1.call-start = ((), (), s32[]{:S(2)}) async-start(), calls=%async_computation.3 | async-start | bytes 184320 | tf_op jit(solution)/shard_map/while/body/eval_jaxpr/reduce_scatter | solution.py:123
  507.5 3.0 collective-permute-start
  577.8 10.6 %all-to-all-start = ((f32[8,4,640]{2,1,0:T(4,128)}), f32[8,4,640]{2,1,0:T(4,128)S(1)}, u32[]{:S(2)}, u32[]{:S(2)}) async-start(f32[8,4,640]{2,1,0:T(4,128)} %all_to_all.47), calls=%async_computation.1 | async-start | bytes 163840 | tf_op jit(solution)/shard_map/while/body/eval_jaxpr/all_to_all | solution.py:133
  632.0 71.3 %reduce-scatter.2.cloned.1.call-start = ((), (), s32[]{:S(2)}) async-start(), calls=%async_computation.3 | async-start | bytes 184320 | tf_op jit(solution)/shard_map/while/body/eval_jaxpr/reduce_scatter | solution.py:123
  632.0 3.0 collective-permute-start
  704.9 10.7 %all-to-all-start = ((f32[8,4,640]{2,1,0:T(4,128)}), f32[8,4,640]{2,1,0:T(4,128)S(1)}, u32[]{:S(2)}, u32[]{:S(2)}) async-start(f32[8,4,640]{2,1,0:T(4,128)} %all_to_all.47), calls=%async_computation.1 | async-start | bytes 163840 | tf_op jit(solution)/shard_map/while/body/eval_jaxpr/all_to_all | solution.py:133
  758.8 67.5 %reduce-scatter.2.cloned.1.call-start = ((), (), s32[]{:S(2)}) async-start(), calls=%async_computation.3 | async-start | bytes 184320 | tf_op jit(solution)/shard_map/while/body/eval_jaxpr/reduce_scatter | solution.py:123
  758.8 3.0 collective-permute-start
  827.9 10.7 %all-to-all-start = ((f32[8,4,640]{2,1,0:T(4,128)}), f32[8,4,640]{2,1,0:T(4,128)S(1)}, u32[]{:S(2)}, u32[]{:S(2)}) async-start(f32[8,4,640]{2,1,0:T(4,128)} %all_to_all.47), calls=%async_computation.1 | async-start | bytes 163840 | tf_op jit(solution)/shard_map/while/body/eval_jaxpr/all_to_all | solution.py:133
  881.8 31.8 %all-reduce.3.cloned.1.call-start = ((), (), s32[]{:S(2)}) async-start(), calls=%async_computation.2 | async-start | bytes 131072 | tf_op jit(solution)/shard_map/psum | solution.py:24
Sparse Core Ops, SparseCore 0:
  24.2 58.8 reduce-scatter.1
  153.3 51.4 reduce-scatter.1
  275.0 51.4 reduce-scatter.1
  395.2 55.9 reduce-scatter.1
  517.0 59.1 reduce-scatter.1
  641.5 61.7 reduce-scatter.1
  768.3 57.9 reduce-scatter.1
Sparse Core Ops, SparseCore 1:
  884.6 28.9 all-reduce.2
